TPU v7x, 256 devices: a whole 4x4x8 slice. The times are simulated.
256 devices in a mesh: rep: 32 (over y_lo, z, core), tp: 8 (over y_hi, x).
Axes of the slice: x: 4, y: 4 (y_hi: 2, y_lo: 2; y = y_hi * 2 + y_lo), z: 8, core: 2. Of those that a mesh axis runs over, the one named last changes fastest.
Arguments:
- positions: int32 [8192], P('rep'), may hold values from 0 to 8191
- activations: bfloat16 [8192, 4096], P('rep', 'tp'), may hold values from -6 to 6
- norm_gain: bfloat16 [4096], P('tp'), may hold values from 0.5 to 1.5
- qkv_weight: bfloat16 [4096, 6144], P('rep', 'tp'), may hold values from -0.09375 to 0.09375
- gate_up_weight: bfloat16 [4096, 14336], P('rep', 'tp'), may hold values from -0.09375 to 0.09375
Outputs:
- qkv_out: bfloat16 [8192, 6144], P('rep', 'tp')
- hidden: bfloat16 [8192, 7168], P('rep', 'tp')
All inputs are finite; a program needn't handle non-finite values.
Results may differ from a plain program's by a relative error of at most 0.0058.
Values may be sent and summed in bfloat16 or wider, within the bound.
A program may use at most 128 MiB of HBM per device.

v0:
```python
import jax
import jax.numpy as jnp
from jax import lax
from jax.sharding import PartitionSpec as P

QH = 32
KVH = 8
HD = 128


theta_base = 500000.0
norm_eps = 1e-05


def in_order(tiles, dim):
    tiles = jnp.moveaxis(tiles, 0, dim)
    shape = tiles.shape
    return tiles.reshape(*shape[:dim], shape[dim] * shape[dim + 1], *shape[dim + 2 :])


def copy_for_each(x, axis):
    devices = lax.axis_size(axis)
    return lax.all_to_all(jnp.broadcast_to(x[None], (devices, *x.shape)), axis, 0, 0, tiled=True)


def collect(x, axis, dim):
    return in_order(copy_for_each(x, axis), dim)


def normalize(gathered, gain_row):
    values = gathered.astype(jnp.float32)
    mean_square = jnp.mean(values * values, axis=1, keepdims=True)
    return (values * lax.rsqrt(mean_square + norm_eps) * gain_row.astype(jnp.float32)).astype(
        jnp.bfloat16
    )


def rotary(joined_qkv, positions):
    row_count = joined_qkv.shape[0]
    per_group = QH // KVH + 2
    half_size = HD // 2
    head_view = joined_qkv.reshape(row_count, -1, per_group, HD)
    frequency = theta_base ** (-2.0 * jnp.arange(half_size, dtype=jnp.float32) / HD)
    angles = positions.astype(jnp.float32)[:, None] * frequency[None, :]
    cosine = jnp.cos(angles)[:, None, None, :]
    sine_part = jnp.sin(angles)[:, None, None, :]
    leading = head_view[..., :half_size]
    trailing = head_view[..., half_size:]
    turned = jnp.concatenate(
        [leading * cosine - trailing * sine_part, trailing * cosine + leading * sine_part], axis=-1
    )
    rotated_mask = (jnp.arange(per_group) < per_group - 1)[None, None, :, None]
    return jnp.where(rotated_mask, turned, head_view).reshape(row_count, -1)


def contract_rows(chosen, piece):
    return jnp.dot(chosen, piece, preferred_element_type=jnp.float32)


def per_device(positions, activations, norm_gain, qkv_weight, gate_up_weight):
    features, gains = (collect(activations, "tp", 1), collect(norm_gain, "tp", 0))
    normed = normalize(features, gains)
    seq_count = normed.shape[0]
    qkv_partial = contract_rows(normed, lax.all_gather(qkv_weight, "rep", axis=0, tiled=True))
    gateup_partial = contract_rows(
        normed, lax.all_gather(gate_up_weight, "rep", axis=0, tiled=True)
    )
    qkv_out = rotary(qkv_partial, positions).astype(jnp.bfloat16)
    paired = gateup_partial.reshape(seq_count, 2, -1)
    hidden = (jax.nn.silu(paired[:, 0]) * paired[:, 1]).astype(jnp.bfloat16)
    return (qkv_out, hidden)


def solution(mesh):
    placed = (P("rep"), P("rep", "tp"), P("tp"), P("rep", "tp"), P("rep", "tp"))
    return jax.shard_map(
        per_device,
        mesh=mesh,
        in_specs=placed,
        out_specs=(P("rep", "tp"), P("rep", "tp")),
        check_vma=False,
    )
```

profile of v0, /device:TPU:1, one launch (start us, length us, event | category | flops | bytes accessed | tf_op | source)
XLA Modules:
  0.0 226.5 jit_solution(5705685493646829225)
XLA Ops:
  7.2 0.0 copy-start.1
  7.2 0.0 all-gather.3.cloned.1.call-start
  7.2 0.7 all-gather.3.cloned.1.call-update
  7.9 0.0 all-gather.5.cloned.1.call-start
  8.0 0.7 all-gather.5.cloned.1.call-update
  8.7 0.7 broadcast_in_dim.17
  9.4 0.5 broadcast.80
  9.9 0.7 reduce.2
  10.6 13.8 %all_to_all.11 = bf16[8,2,256]{2,1,0:T(2,128)(2,1)S(1)} all-to-all(bf16[8,2,256]{2,1,0:T(2,128)(2,1)S(1)} %reshape.127), channel_id=1, replica_groups=mesh['rep'=32,'tp'=8] {'tp'}, dimensions={0} | all-to-all | bytes 16384 | tf_op jit(solution)/shard_map/all_to_all | solution.py:23
  24.4 2.5 %broadcast_in_dim.16 = bf16[8,256,512]{2,1,0:T(8,128)(2,1)} broadcast(bf16[256,512]{1,0:T(8,128)(2,1)} %param.6), dimensions={1,2} | broadcast | bytes 2359296 | tf_op jit(solution)/shard_map/broadcast_in_dim | solution.py:23
  26.9 4.4 %all-to-all-start = ((bf16[8,256,512]{2,1,0:T(8,128)(2,1)}), bf16[8,256,512]{2,1,0:T(8,128)(2,1)}, u32[]{:S(2)}, u32[]{:S(2)}) async-start(bf16[8,256,512]{2,1,0:T(8,128)(2,1)} %broadcast_in_dim.16), calls=%async_computation | async-start | bytes 4194304 | tf_op jit(solution)/shard_map/all_to_all | solution.py:23
  31.2 0.0 copy-done.1
  31.3 0.1 broadcast_bitcast_fusion
  31.4 0.3 multiply_cosine_fusion
  31.7 28.9 %all-to-all-done = bf16[8,256,512]{2,1,0:T(8,128)(2,1)} async-done(((bf16[8,256,512]{2,1,0:T(8,128)(2,1)}), bf16[8,256,512]{2,1,0:T(8,128)(2,1)}, u32[]{:S(2)}, u32[]{:S(2)}) %all-to-all-start) | async-done | bytes 2097184 | tf_op jit(solution)/shard_map/all_to_all | solution.py:23
  60.6 2.9 %copy.14 = bf16[8,256,512]{1,2,0:T(8,128)(2,1)S(1)} copy(bf16[8,256,512]{2,1,0:T(8,128)(2,1)} %all-to-all-done) | data formatting | bytes 4194304 | tf_op jit(solution)/shard_map/all_to_all | solution.py:23
  63.5 0.6 multiply_reduce_fusion
  64.1 1.7 multiply_convert_fusion
  65.8 1.7 fusion.1
  67.5 32.9 %all-gather.3.cloned.1.call-done = bf16[4096,768]{1,0:T(8,128)(2,1)} async-done(((bf16[128,768]{1,0:T(8,128)(2,1)}), bf16[4096,768]{1,0:T(8,128)(2,1)}) %all-gather.3.cloned.1.call-update) | async-done | bytes 6291472 | tf_op jit(solution)/shard_map/all_gather | solution.py:64
  100.4 5.2 %fusion.4 = f32[256,768]{1,0:T(8,128)S(1)} fusion(bf16[256,4096]{0,1:T(8,128)(2,1)} %fusion.1, bf16[4096,768]{1,0:T(8,128)(2,1)} %all-gather.3.cloned.1.call-done), kind=kOutput, calls=%fused_computation.20 | convolution fusion | flops 1610612736 | bytes 9175040 | tf_op jit(solution)/shard_map/dot_general | solution.py:57
  105.6 0.3 copy.15
  105.9 0.1 multiply_subtract_fusion
  106.0 0.2 copy.16
  106.2 0.8 select_convert_fusion
  107.0 83.8 %all-gather.5.cloned.1.call-done = bf16[4096,1792]{1,0:T(8,128)(2,1)} async-done(((bf16[128,1792]{1,0:T(8,128)(2,1)}), bf16[4096,1792]{1,0:T(8,128)(2,1)}) %all-gather.5.cloned.1.call-update) | async-done | bytes 14680080 | tf_op jit(solution)/shard_map/all_gather | solution.py:66
  190.9 0.0 copy-start
  190.9 19.8 %copy.17 = bf16[1792,4096]{1,0:T(8,128)(2,1)} copy(bf16[1792,4096]{0,1:T(8,128)(2,1)} %bitcast.37) | data formatting | bytes 29360128 | tf_op jit(solution)/shard_map/dot_general | solution.py:57
  210.7 0.0 copy-done
  210.7 7.9 %fusion.5 = f32[256,2,896]{2,0,1:T(8,128)S(1)} fusion(bf16[256,4096,1]{0,1,2:T(8,128)(2,1)S(1)} %bitcast.40, bf16[2,896,4096]{2,1,0:T(8,128)(2,1)} %bitcast.38), kind=kOutput, calls=%fused_computation.21 | convolution fusion | flops 3758096384 | bytes 18612224 | tf_op jit(solution)/shard_map/dot_general | solution.py:57
  218.6 1.0 fusion.3
  (9 shorter events, 0.1 us)
Async XLA Ops:
  7.2 24.1 %copy-start.1 = (s32[256]{0:T(256)S(1)}, s32[256]{0:T(256)}, u32[]{:S(2)}) copy-start(s32[256]{0:T(256)} %param.5) | copy-start | bytes 3076
  7.2 93.2 %all-gather.3.cloned.1.call-start = ((), (), s32[]{:S(2)}) async-start(), calls=%async_computation.2 | async-start | bytes 6488064 | tf_op jit(solution)/shard_map/all_gather | solution.py:64
  7.9 183.0 %all-gather.5.cloned.1.call-start = ((), (), s32[]{:S(2)}) async-start(), calls=%async_computation.3 | async-start | bytes 15138816 | tf_op jit(solution)/shard_map/all_gather | solution.py:66
  26.9 33.8 %all-to-all-start = ((bf16[8,256,512]{2,1,0:T(8,128)(2,1)}), bf16[8,256,512]{2,1,0:T(8,128)(2,1)}, u32[]{:S(2)}, u32[]{:S(2)}) async-start(bf16[8,256,512]{2,1,0:T(8,128)(2,1)} %broadcast_in_dim.16), calls=%async_computation | async-start | bytes 4194304 | tf_op jit(solution)/shard_map/all_to_all | solution.py:23
  190.9 19.8 %copy-start = (bf16[8,256,512]{1,2,0:T(8,128)(2,1)S(1)}, bf16[8,256,512]{1,2,0:T(8,128)(2,1)}, u32[]{:S(2)}) copy-start(bf16[8,256,512]{1,2,0:T(8,128)(2,1)} %multiply_convert_fusion) | copy-start | bytes 6291460
Sparse Core Ops, SparseCore 0:
  9.8 90.4 all-gather.2
  102.2 88.6 all-gather.4
where the time goes:
time: 227 us; the launch traced here: 226 us
  waiting for transfers between devices  147 us (65%)
  local copies, waits for them, and re-layouts  26.9 us (12%)
  between operations  14.2 us (6%)
  blocking collectives  13.8 us (6%)
  matrix products  13.1 us (6%)
  other arithmetic  7.03 us (3%)
  starting transfers between devices  4.44 us (2%)
    all_gather x1, waiting for transfers between devices, per_device(): lax.all_gather(gate_up_weight, 'rep', axis=0, tiled=True)  83.8 us
    all_gather x1, waiting for transfers between devices, per_device(): lax.all_gather(qkv_weight, 'rep', axis=0, tiled=True)  32.9 us
    all_to_all x1, waiting for transfers between devices, copy_for_each(): lax.all_to_all(jnp.broadcast_to(x[None], (devices, *x.shape)), axis, 0, 0...  28.9 us
    dot_general x2, local copies, waits for them, and re-layouts, contract_rows(): return jnp.dot(chosen, piece, preferred_element_type=jnp.float32)  20.1 us
    all_to_all x1, blocking collectives, copy_for_each(): lax.all_to_all(jnp.broadcast_to(x[None], (devices, *x.shape)), axis, 0, 0...  13.8 us
    dot_general x2, matrix products, contract_rows(): return jnp.dot(chosen, piece, preferred_element_type=jnp.float32)  13.1 us
  transfers between devices with their start and end apart: 3, of which 3 were waited for; matrix products, arithmetic and copies ran while one was open for 8% of the time, Pallas kernels for 0%

commit v1 on v0

v1 whole, which is shorter than its diff:
```python
import jax
import jax.numpy as jnp
from jax import lax
from jax.experimental import pallas as pl
from jax.experimental.pallas import tpu as pltpu
from jax.sharding import PartitionSpec as P

HD = 128
theta_base = 500000.0
norm_eps = 1e-05

MESH = pl.DeviceIdType.MESH
NB = 5
FIRST = 3
OFF = (0, 3, 1, 2)
COLORS = (("x", "y", 1), ("x", "y", -1), ("y", "x", 1), ("y", "x", -1), ("x", "y", 1))


def kernel(
    cs_ref, x_ref, g_ref, wq_ref, wg_ref, oq_ref, oh_ref,
    S, W, A, G, N, T, ACC, OS,
    ld_sem, z_send, z_recv, d_send, d_recv, ye_send, ye_recv,
    a_send, a_recv, t_sem, o_send, o_recv, o_loc,
):
    rep = lax.axis_index("rep")
    tp = lax.axis_index("tp")
    core = rep % 2
    z = (rep // 2) % 8
    yl = rep // 16
    x = tp % 4
    y = (tp // 4) * 2 + yl

    def dev(xx, yy, zz, cc):
        return (((yy % 2) * 8 + zz) * 2 + cc, (yy // 2) * 4 + xx)

    xp, xm = dev((x + 1) % 4, y, z, core), dev((x + 3) % 4, y, z, core)
    yp, ym = dev(x, (y + 1) % 4, z, core), dev(x, (y + 3) % 4, z, core)
    zp, zm = dev(x, y, (z + 1) % 8, core), dev(x, y, (z + 7) % 8, core)
    pc = dev(x, y, z, 1 - core)
    yo = (((1 - yl) * 8 + z) * 2 + core, tp)
    step_to = {("x", 1): xp, ("x", -1): xm, ("y", 1): yp, ("y", -1): ym}

    barrier = pltpu.get_barrier_semaphore()
    for d in (xp, xm, yp, ym, zp, zm, pc):
        pl.semaphore_signal(barrier, inc=1, device_id=d, device_id_type=MESH)

    act_load = pltpu.make_async_copy(x_ref, A.at[tp, pl.ds(yl * 256, 256), :], ld_sem.at[1])
    act_load.start()
    gain_load = pltpu.make_async_copy(g_ref, G.at[tp, yl], ld_sem.at[2])
    gain_load.start()
    for s, c in ((0, 0), (5, 256), (6, 512)):
        pltpu.make_async_copy(wq_ref.at[:, pl.ds(c, 256)], S.at[s], ld_sem.at[0]).start()
    for p in range(7):
        s = p + 1 if p < 4 else p + 3
        for side in range(2):
            pltpu.make_async_copy(
                wg_ref.at[:, pl.ds(side * 896 + p * 128, 128)],
                S.at[s, :, pl.ds(side * 128, 128)],
                ld_sem.at[0],
            ).start()
    t_load = pltpu.make_async_copy(cs_ref, T.at[yl], ld_sem.at[3])
    t_load.start()

    def remote(src, dst, ssem, rsem, to):
        return pltpu.make_async_remote_copy(
            src_ref=src, dst_ref=dst, send_sem=ssem, recv_sem=rsem, device_id=to, device_id_type=MESH
        )

    def w_at(b, py, pz, pcore):
        return W.at[b, py * 8 + pz, pl.ds(pcore * 128, 128), :]

    def plane(s):
        return yl if s == 0 else 1 - yl

    def z_copy(b, s, dr, h, own=False):
        src_z = (z - dr * (h - 1) + 8) % 8
        ref = w_at(b, plane(s), src_z, core)
        src = S.at[yl * NB + b] if own else ref
        i = (((0 if dr == 1 else 1) * 4 + (h - 1)) * 2 + s) * NB + b
        return remote(src, ref, z_send.at[i], z_recv.at[i], zp if dr == 1 else zm)

    def z_wait(b, s, dr, h):
        src_z = (z - dr * h + 8) % 8
        ref = w_at(b, plane(s), src_z, core)
        i = (((0 if dr == 1 else 1) * 4 + (h - 1)) * 2 + s) * NB + b
        remote(ref, ref, z_send.at[i], z_recv.at[i], zp if dr == 1 else zm).wait_recv()

    def d_copy(b, s, j, own=False):
        src_z = (z + j + 8) % 8
        ref = w_at(b, plane(s), src_z, core)
        src = S.at[yl * NB + b] if own else ref
        i = ((j + 3) * 2 + s) * NB + b
        return remote(src, ref, d_send.at[i], d_recv.at[i], pc)

    def d_wait(b, s, j):
        src_z = (z + j + 8) % 8
        ref = w_at(b, plane(s), src_z, 1 - core)
        i = ((j + 3) * 2 + s) * NB + b
        remote(ref, ref, d_send.at[i], d_recv.at[i], pc).wait_recv()

    def a_at(c, o1, o2):
        ox, oy = (o1, o2) if COLORS[c][0] == "x" else (o2, o1)
        xx = (x + OFF[ox]) % 4
        yy = (y + OFF[oy]) % 4
        t = (yy // 2) * 4 + xx
        if c == 4:
            return G.at[t, yy % 2]
        return A.at[t, pl.ds((yy % 2) * 256 + c * 64, 64), :]

    def a_send_to(c, phase, o1, o2, sign, kind):
        r1, r2 = (kind, o2) if phase == 0 else (o1, kind)
        ref = a_at(c, o1, o2)
        i = c * 16 + r1 * 4 + r2
        return remote(ref, ref, a_send.at[i], a_recv.at[i], step_to[(COLORS[c][phase], sign)])

    def a_both(c, phase, o1, o2):
        a_send_to(c, phase, o1, o2, 1, 1).start()
        a_send_to(c, phase, o1, o2, -1, 2).start()

    def a_relay(c, phase, o1, o2):
        a_send_to(c, phase, o1, o2, COLORS[c][2], 3).start()

    def a_wait(c, o1, o2):
        ref = a_at(c, o1, o2)
        i = c * 16 + o1 * 4 + o2
        remote(ref, ref, a_send.at[i], a_recv.at[i], xp).wait_recv()

    def long_kind(c):
        return 1 if COLORS[c][2] == 1 else 2

    def short_kind(c):
        return 2 if COLORS[c][2] == 1 else 1

    def blocks(lo, hi, f):
        def body(b, carry):
            f(b)
            return carry

        lax.fori_loop(lo, hi, body, 0)

    act_load.wait()
    gain_load.wait()
    pl.semaphore_wait(barrier, 7)

    for c in (2, 3, 0, 1, 4):
        a_both(c, 0, 0, 0)
    pltpu.make_async_copy(S, S, ld_sem.at[0]).wait()

    def start_own(b):
        z_copy(b, 0, 1, 1, own=True).start()
        z_copy(b, 0, -1, 1, own=True).start()
        remote(
            S.at[(1 - yl) * NB + b], w_at(b, yl, z, core), ye_send.at[b], ye_recv.at[b], yo
        ).start()
        d_copy(b, 0, 0, own=True).start()

    blocks(0, NB, start_own)
    for c in (0, 1, 4, 2, 3):
        a_both(c, 1, 0, 0)

    def keep_own(b):
        W[b, yl * 8 + z, pl.ds(core * 128, 128), :] = S[yl * NB + b]

    blocks(0, NB, keep_own)

    for c in (2, 3, 0, 1, 4):
        o = long_kind(c)
        a_wait(c, o, 0)
        a_relay(c, 0, o, 0)
        a_both(c, 1, o, 0)
    for c in (2, 3, 0, 1, 4):
        o = short_kind(c)
        a_wait(c, o, 0)
        a_both(c, 1, o, 0)

    def start_other(b):
        ref = w_at(b, 1 - yl, z, core)
        remote(ref, ref, ye_send.at[b], ye_recv.at[b], yo).wait_recv()
        z_copy(b, 1, 1, 1).start()
        z_copy(b, 1, -1, 1).start()
        d_copy(b, 1, 0).start()

    blocks(0, NB, start_other)

    for c in (2, 3, 0, 1, 4):
        a_wait(c, 3, 0)
        a_both(c, 1, 3, 0)

    def arrive(h, s, forward):
        def f(b):
            for dr in (1, -1):
                if h == 4 and (dr == 1) != (s == 0):
                    continue
                z_wait(b, s, dr, h)
                if forward and not (h == 3 and (dr == 1) != (s == 0)):
                    z_copy(b, s, dr, h + 1).start()
                d_copy(b, s, 4 if h == 4 else -dr * h).start()

        return f

    def second_relays(o1):
        for c in (0, 1, 2, 3, 4):
            a_wait(c, o1, long_kind(c))
            a_relay(c, 1, o1, long_kind(c))

    blocks(0, FIRST, arrive(1, 0, True))
    second_relays(0)
    blocks(0, FIRST, arrive(1, 1, True))
    for o1 in (1, 2):
        second_relays(o1)
    blocks(FIRST, NB, arrive(1, 0, False))
    blocks(FIRST, NB, arrive(1, 1, False))
    second_relays(3)
    blocks(0, FIRST, arrive(2, 0, True))
    blocks(0, FIRST, arrive(2, 1, True))
    t_load.wait()
    t_copy = remote(T.at[yl], T.at[yl], t_sem.at[0], t_sem.at[1], yo)
    t_copy.start()
    blocks(0, FIRST, arrive(3, 0, True))
    for o1 in (0, 1, 2, 3):
        for c in (0, 1, 2, 3, 4):
            a_wait(c, o1, short_kind(c))
            a_wait(c, o1, 3)

    def norm_rows(i, carry):
        rows = pl.ds(i * 32, 32)
        total = jnp.zeros((32, 128), jnp.float32)
        for t in range(8):
            v = A[t, rows, :].astype(jnp.float32)
            v = v * v
            total = total + ((v[:, 0:128] + v[:, 128:256]) + (v[:, 256:384] + v[:, 384:512]))
        mean_square = jnp.sum(total, axis=1, keepdims=True) * (1.0 / 4096.0)
        scale = lax.rsqrt(mean_square + norm_eps)
        for t in range(8):
            v = A[t, rows, :].astype(jnp.float32)
            g = G[t, 0].astype(jnp.float32)
            v = (v * scale * g).astype(jnp.bfloat16)
            N[2 * t, rows, :] = v[:, 0:256]
            N[2 * t + 1, rows, :] = v[:, 256:512]
        return carry

    lax.fori_loop(0, 16, norm_rows, 0)

    blocks(0, FIRST, arrive(3, 1, True))

    def forward_second(s):
        def f(b):
            z_copy(b, s, 1, 2).start()
            z_copy(b, s, -1, 2).start()

        return f

    for s in range(2):
        blocks(FIRST, NB, forward_second(s))

    def compute(js, first):
        def f(b):
            for j in js:
                for s in range(2):
                    d_wait(b, s, j)

            def body(m, carry):
                rows = pl.ds(m * 256, 256)
                total = None if first else ACC[b, rows, :]
                for j in js:
                    zz = (z + j + 8) % 8
                    for half in range(2):
                        k = half * 8 + zz
                        part = jnp.dot(N[k, rows, :], W[b, k], preferred_element_type=jnp.float32)
                        total = part if total is None else total + part
                ACC[b, rows, :] = total
                return carry

            lax.fori_loop(0, 2, body, 0)

        return f

    lane = lax.broadcasted_iota(jnp.int32, (32, 128), 1)

    def pair_rows(b):
        def body(i, carry):
            rows = pl.ds(i * 32, 32)
            gate = ACC[b, rows, 0:128]
            up = ACC[b, rows, 128:256]
            OS[b, rows, 0:128] = (gate / (1.0 + jnp.exp(-gate)) * up).astype(jnp.bfloat16)
            return carry

        lax.fori_loop(0, 16, body, 0)

    def head_rows(b):
        def body(i, carry):
            rows = pl.ds(i * 32, 32)
            table = T[i // 8, pl.ds((i % 8) * 32, 32), :]
            turned = pltpu.roll(table, 64, 1)
            cosine = jnp.where(lane < 64, table, turned)
            sine = jnp.where(lane < 64, -turned, table)
            for head in range(2):
                v = ACC[b, rows, pl.ds(head * 128, 128)]
                r = v * cosine + pltpu.roll(v, 64, 1) * sine
                if b == 1 and head == 1:
                    r = v
                OS[b, rows, pl.ds(head * 128, 128)] = r.astype(jnp.bfloat16)
            return carry

        lax.fori_loop(0, 16, body, 0)

    def is_head(b, half, then, other):
        if b == 0:
            then()
        elif b == 1:
            pl.when(half == 1)(then)
            pl.when(half == 0)(other)
        else:
            other()

    def out_slices(b, half, head):
        if head:
            at = oq_ref.at[:, pl.ds(pl.multiple_of(256 * (b + half), 256), 256)]
        else:
            at = oh_ref.at[:, pl.ds(pl.multiple_of(128 * (b - 1 + 3 * half), 128), 128)]
        return at, 256 if head else 128

    def out_copies(b, head):
        at, width = out_slices(b, yl, head)
        away = remote(
            OS.at[b, pl.ds((1 - yl) * 256, 256), pl.ds(0, width)], at, o_send.at[b], o_recv.at[b], yo
        )
        here = pltpu.make_async_copy(OS.at[b, pl.ds(yl * 256, 256), pl.ds(0, width)], at, o_loc.at[b])
        return away, here

    def finish(b):
        def go(head):
            def f():
                (head_rows if head else pair_rows)(b)
                away, here = out_copies(b, head)
                away.start()
                here.start()

            return f

        is_head(b, yl, go(True), go(False))

    blocks(0, FIRST, compute((0, -1, 1, -2, 2), True))
    for s in range(2):
        blocks(0, FIRST, arrive(4, s, False))
    blocks(FIRST, NB, arrive(2, 0, True))
    blocks(0, FIRST, compute((-3, 3, 4), False))
    blocks(FIRST, NB, arrive(2, 1, True))
    remote(T.at[1 - yl], T.at[1 - yl], t_sem.at[0], t_sem.at[1], yo).wait_recv()
    for b in range(FIRST):
        finish(b)
    blocks(FIRST, NB, compute((0, -1, 1, -2, 2), True))
    for s in range(2):
        blocks(FIRST, NB, arrive(3, s, True))
    blocks(FIRST, NB, compute((-3, 3), False))
    for s in range(2):
        blocks(FIRST, NB, arrive(4, s, False))
    for b in range(FIRST, NB):
        compute((4,), False)(b)
        finish(b)

    t_copy.wait_send()

    def sent(b):
        ref = S.at[b]
        for s in range(2):
            for dr in range(2):
                for h in range(4):
                    if h == 3 and dr != s:
                        continue
                    i = ((dr * 4 + h) * 2 + s) * NB + b
                    remote(ref, ref, z_send.at[i], z_recv.at[i], zp).wait_send()
            for j in range(8):
                i = (j * 2 + s) * NB + b
                remote(ref, ref, d_send.at[i], d_recv.at[i], pc).wait_send()
        remote(ref, ref, ye_send.at[b], ye_recv.at[b], yo).wait_send()

    blocks(0, NB, sent)
    for c in range(5):
        for o1 in range(4):
            for o2 in range(4):
                if o1 or o2:
                    ref = a_at(c, 0, 0)
                    i = c * 16 + o1 * 4 + o2
                    remote(ref, ref, a_send.at[i], a_recv.at[i], xp).wait_send()

    for b in range(NB):

        def out_sent(head):
            def f():
                away, here = out_copies(b, head)
                here.wait()
                away.wait_send()

            return f

        is_head(b, yl, out_sent(True), out_sent(False))

        def out_arrived(head):
            def f():
                at, _ = out_slices(b, 1 - yl, head)
                remote(at, at, o_send.at[b], o_recv.at[b], yo).wait_recv()

            return f

        is_head(b, 1 - yl, out_arrived(True), out_arrived(False))


def per_device(positions, activations, norm_gain, qkv_weight, gate_up_weight):
    half_size = HD // 2
    frequency = theta_base ** (-2.0 * jnp.arange(half_size, dtype=jnp.float32) / HD)
    angles = positions.astype(jnp.float32)[:, None] * frequency[None, :]
    table = jnp.concatenate([jnp.cos(angles), jnp.sin(angles)], axis=1)
    sems = pltpu.SemaphoreType.DMA
    return pl.pallas_call(
        kernel,
        out_shape=(
            jax.ShapeDtypeStruct((256, 768), jnp.bfloat16),
            jax.ShapeDtypeStruct((256, 896), jnp.bfloat16),
        ),
        in_specs=[pl.BlockSpec(memory_space=pl.ANY)] * 5,
        out_specs=(pl.BlockSpec(memory_space=pl.ANY),) * 2,
        scratch_shapes=[
            pltpu.VMEM((2 * NB, 128, 256), jnp.bfloat16),
            pltpu.VMEM((NB, 16, 256, 256), jnp.bfloat16),
            pltpu.VMEM((8, 512, 512), jnp.bfloat16),
            pltpu.VMEM((8, 2, 1, 512), jnp.bfloat16),
            pltpu.VMEM((16, 512, 256), jnp.bfloat16),
            pltpu.VMEM((2, 256, 128), jnp.float32),
            pltpu.VMEM((NB, 512, 256), jnp.float32),
            pltpu.VMEM((NB, 512, 256), jnp.bfloat16),
            sems((4,)),
            sems((16 * NB,)),
            sems((16 * NB,)),
            sems((16 * NB,)),
            sems((16 * NB,)),
            sems((NB,)),
            sems((NB,)),
            sems((80,)),
            sems((80,)),
            sems((2,)),
            sems((NB,)),
            sems((NB,)),
            sems((NB,)),
        ],
        compiler_params=pltpu.CompilerParams(
            collective_id=0, has_side_effects=True, vmem_limit_bytes=48 * 1024 * 1024
        ),
    )(table, activations, norm_gain.reshape(1, 512), qkv_weight, gate_up_weight)


def solution(mesh):
    placed = (P("rep"), P("rep", "tp"), P("tp"), P("rep", "tp"), P("rep", "tp"))
    return jax.shard_map(
        per_device,
        mesh=mesh,
        in_specs=placed,
        out_specs=(P("rep", "tp"), P("rep", "tp")),
        check_vma=False,
    )
```

time: 227 us -> 80.1 us (0.35)
  waiting for transfers between devices: 147 us -> 0 us
  Pallas kernels: 0 us -> 73.9 us
  local copies, waits for them, and re-layouts: 26.9 us -> 3.96 us
  blocking collectives: 13.8 us -> 0 us
  between operations: 14.2 us -> 0.68 us
  matrix products: 13.1 us -> 0 us
  other arithmetic: 7.03 us -> 1.37 us
  starting transfers between devices: 4.44 us -> 0 us
    all_gather x2 -> x0, waiting for transfers between devices: 117 us -> none  [the longest x1 83.8 us: per_device(): lax.all_gather(gate_up_weight, 'rep', axis=0, tiled=True)]
    pallas_call x0 -> x1, Pallas kernels: none -> 73.9 us  [per_device(): pl.pallas_call(kernel, out_shape=(jax.ShapeDtypeStruct((256, 768), jnp.bf...]
    all_to_all x1 -> x0, waiting for transfers between devices: 28.9 us -> none  [copy_for_each(): lax.all_to_all(jnp.broadcast_to(x[None], (devices, *x.shape)), axis, 0, 0...]
    dot_general x2 -> x0, local copies, waits for them, and re-layouts: 20.1 us -> none  [contract_rows(): return jnp.dot(chosen, piece, preferred_element_type=jnp.float32)]
    all_to_all x1 -> x0, blocking collectives: 13.8 us -> none  [copy_for_each(): lax.all_to_all(jnp.broadcast_to(x[None], (devices, *x.shape)), axis, 0, 0...]
    dot_general x2 -> x0, matrix products: 13.1 us -> none  [contract_rows(): return jnp.dot(chosen, piece, preferred_element_type=jnp.float32)]
    all_to_all x1 -> x0, starting transfers between devices: 4.36 us -> none  [copy_for_each(): lax.all_to_all(jnp.broadcast_to(x[None], (devices, *x.shape)), axis, 0, 0...]
    broadcast_in_dim x4 -> x0, local copies, waits for them, and re-layouts: 3.75 us -> none  [the longest x3 3.68 us: copy_for_each(): jnp.broadcast_to(x[None], (devices, *x.shape))]
  transfers between devices with their start and end apart: 3 -> 0, of which waited for: 3 -> 0; matrix products, arithmetic and copies ran while one was open for 8% -> 0% of each run, Pallas kernels for 0% -> 0%
where the time goes in v1:
time: 80.1 us; the launch traced here: 79.9 us
  Pallas kernels  73.9 us (92%)
  local copies, waits for them, and re-layouts  3.96 us (5%)
  other arithmetic  1.37 us (2%)
    pallas_call x1, Pallas kernels, per_device(): pl.pallas_call(kernel, out_shape=(jax.ShapeDtypeStruct((256, 768), jnp.bf...  73.9 us
    unnamed x8, local copies, waits for them, and re-layouts  3.27 us

profile of v1, /device:TPU:1, one launch (start us, length us, event | category | flops | bytes accessed | tf_op | source)
XLA Modules:
  0.0 79.9 jit_solution(416471151786420256)
XLA Ops:
  0.6 0.0 copy-start
  0.7 0.7 convert_element_type.3
  1.4 0.7 reshape.13.g_ref
  2.1 0.5 multiply_cosine_fusion
  2.6 0.0 copy-start.2
  2.6 0.1 pad_maximum_fusion.cs_ref
  2.7 0.0 copy-done
  2.7 0.8 %copy-done.2 = bf16[128,768]{1,0:T(8,128)(2,1)S(1)} copy-done((bf16[128,768]{1,0:T(8,128)(2,1)S(1)}, bf16[128,768]{1,0:T(8,128)(2,1)}, u32[]{:S(2)}) %copy-start.2) | copy-done | bytes 196632
  3.5 0.0 copy-start.1
  3.5 0.9 %copy-done.1 = bf16[256,512]{1,0:T(8,128)(2,1)S(1)} copy-done((bf16[256,512]{1,0:T(8,128)(2,1)S(1)}, bf16[256,512]{1,0:T(8,128)(2,1)}, u32[]{:S(2)}) %copy-start.1) | copy-done | bytes 262168
  4.5 73.9 %shard_map.68 = (bf16[256,768]{1,0:T(8,128)(2,1)S(1)}, bf16[256,896]{1,0:T(8,128)(2,1)S(1)}) custom-call(f32[256,128]{1,0:T(8,128)S(1)} %pad_maximum_fusion.cs_ref, bf16[256,512]{1,0:T(8,128)(2,1)S(1)} %copy-done.1, bf16[1,512]{1,0:T(2,128)(2,1)S(1)} %reshape.13.g_ref, bf16[128,768]{1,0:T(8,128)(2,1)S(1)} %copy-done.2, bf16[128,1792]{1,0:T(8,128)(2,1)S(1)} %copy-done), custom_call_target="tpu_custom_call" | custom-call | tf_op jit(solution)/shard_map/pallas_call | solution.py:415
  78.4 0.7 copy.9
  79.1 0.8 copy.10
  (1 shorter events, 0.0 us)
Async XLA Ops:
  0.6 2.1 %copy-start = (bf16[128,1792]{1,0:T(8,128)(2,1)S(1)}, bf16[128,1792]{1,0:T(8,128)(2,1)}, u32[]{:S(2)}) copy-start(bf16[128,1792]{1,0:T(8,128)(2,1)} %wg_ref.1) | copy-start | bytes 1376260
  2.6 0.9 %copy-start.2 = (bf16[128,768]{1,0:T(8,128)(2,1)S(1)}, bf16[128,768]{1,0:T(8,128)(2,1)}, u32[]{:S(2)}) copy-start(bf16[128,768]{1,0:T(8,128)(2,1)} %wq_ref.1) | copy-start | bytes 589828
  3.5 0.9 %copy-start.1 = (bf16[256,512]{1,0:T(8,128)(2,1)S(1)}, bf16[256,512]{1,0:T(8,128)(2,1)}, u32[]{:S(2)}) copy-start(bf16[256,512]{1,0:T(8,128)(2,1)} %x_ref.1) | copy-start | bytes 786436
